TPU v7x, 32 devices: a whole 2x2x4 slice. The times are simulated.
32 devices in a mesh: dp: 8 (over y, x, core), tensor: 4 (over z).
Axes of the slice: x: 2, y: 2, z: 4, core: 2. Of those that a mesh axis runs over, the one named last changes fastest.
Arguments:
- inputs: bfloat16 [2048, 2048], P('dp'), may hold values from -6 to 6
- ln_gain: float32 [2048], replicated, may hold values from 0.5 to 1.5
- ln_bias: float32 [2048], replicated, may hold values from -1.75 to 1.75
- w_qkv: bfloat16 [2048, 6144], P(None, 'tensor'), may hold values from -1 to 1
- b_qkv: float32 [6144], P('tensor'), may hold values from -1.75 to 1.75
- w_out: bfloat16 [2048, 2048], P('tensor'), may hold values from -0.75 to 0.75
- b_out: float32 [2048], replicated, may hold values from -1.75 to 1.75
- w_fc1: bfloat16 [2048, 8192], P(None, 'tensor'), may hold values from -0.125 to 0.125
- b_fc1: float32 [8192], P('tensor'), may hold values from -3 to 3
- w_fc2: bfloat16 [8192, 2048], P('tensor'), may hold values from -0.0625 to 0.0625
- b_fc2: float32 [2048], replicated, may hold values from -1.75 to 1.75
- cotangent: bfloat16 [2048, 2048], P('dp')
Outputs:
- output: bfloat16 [2048, 2048], P('dp')
- input_grad: float32 [2048, 2048], P('dp')
- grad_ln_gain: float32 [2048], replicated
- grad_ln_bias: float32 [2048], replicated
- grad_w_qkv: float32 [2048, 6144], P(None, 'tensor')
- grad_b_qkv: float32 [6144], P('tensor')
- grad_w_out: float32 [2048, 2048], P('tensor')
- grad_b_out: float32 [2048], replicated
- grad_w_fc1: float32 [2048, 8192], P(None, 'tensor')
- grad_b_fc1: float32 [8192], P('tensor')
- grad_w_fc2: float32 [8192, 2048], P('tensor')
- grad_b_fc2: float32 [2048], replicated
All inputs are finite; a program needn't handle non-finite values.
Results may differ from a plain program's by a relative error of at most 0.02.
Values may be sent and summed in bfloat16 or wider, within the bound.
A program may use at most 320 MiB of HBM per device.

v0:
```python
import jax
import jax.numpy as jnp
from jax import lax
from jax.sharding import PartitionSpec as P

HD = 64
ROT = 32
EPS = 1e-05
GELU_C = 0.7978845608028654
GELU_A = 0.044715


def gelu(argument):
    inner = GELU_C * (argument + GELU_A * argument * argument * argument)
    return 0.5 * argument * (1.0 + jnp.tanh(inner))


def gelu_slope(argument):
    tangent = jnp.tanh(GELU_C * (argument + GELU_A * argument * argument * argument))
    return 0.5 * (1.0 + tangent) + 0.5 * argument * (1.0 - tangent * tangent) * GELU_C * (
        1.0 + 3.0 * GELU_A * argument * argument
    )


def rotary_tables(length):
    position = jnp.arange(length).astype(jnp.float32)
    freqs = 10000.0 ** (-(jnp.arange(ROT // 2).astype(jnp.float32) * 2.0 / ROT))
    angles = position[:, None] * freqs[None, :]
    return (jnp.cos(angles)[:, None, :], jnp.sin(angles)[:, None, :])


def rotate(tensor, cosine, sine):
    first = tensor[..., : ROT // 2]
    second = tensor[..., ROT // 2 : ROT]
    return jnp.concatenate(
        [first * cosine - second * sine, second * cosine + first * sine, tensor[..., ROT:]], axis=-1
    )


def unrotate(grad, cosine, sine):
    first = grad[..., : ROT // 2]
    second = grad[..., ROT // 2 : ROT]
    return jnp.concatenate(
        [first * cosine + second * sine, second * cosine - first * sine, grad[..., ROT:]], axis=-1
    )


def probabilities(query_rot, key_rot, logsum):
    length = query_rot.shape[0]
    scores = jnp.einsum(
        "qhd,khd->hqk", query_rot, key_rot, preferred_element_type=jnp.float32
    ) * HD ** (-0.5)
    causal = jnp.arange(length)[:, None] >= jnp.arange(length)[None, :]
    scores = jnp.where(causal[None], scores, -1e30)
    top = jnp.max(scores, -1, keepdims=True)
    logsum = top + jnp.log(jnp.sum(jnp.exp(scores - top), -1, keepdims=True))
    return (jnp.exp(scores - logsum), logsum)


def per_device(
    inputs, ln_gain, ln_bias, w_qkv, b_qkv, w_out, b_out, w_fc1, b_fc1, w_fc2, b_fc2, cotangent
):
    length = inputs.shape[0]
    heads = w_out.shape[0] // HD
    cosine, sine = rotary_tables(length)
    widened = inputs.astype(jnp.float32)
    average = jnp.mean(widened, -1, keepdims=True)
    centered = widened - average
    inv_std = lax.rsqrt(jnp.mean(centered * centered, -1, keepdims=True) + EPS)
    normed_hat = centered * inv_std
    normed = (normed_hat * ln_gain + ln_bias).astype(jnp.bfloat16)
    projected = (jnp.dot(normed, w_qkv, preferred_element_type=jnp.float32) + b_qkv).reshape(
        length, heads, 3, HD
    )
    query_rot = rotate(projected[:, :, 0], cosine, sine).astype(jnp.bfloat16)
    key_rot = rotate(projected[:, :, 1], cosine, sine).astype(jnp.bfloat16)
    value_bf = projected[:, :, 2].astype(jnp.bfloat16)
    probs, logsum = probabilities(query_rot, key_rot, None)
    prob_bf = probs.astype(jnp.bfloat16)
    attended = jnp.einsum("hqk,khd->qhd", prob_bf, value_bf, preferred_element_type=jnp.float32)
    attended = attended.astype(jnp.bfloat16).reshape(length, heads * HD)
    hidden_pre = jnp.dot(normed, w_fc1, preferred_element_type=jnp.float32) + b_fc1
    activated = gelu(hidden_pre).astype(jnp.bfloat16)
    partial_value = jnp.dot(attended, w_out, preferred_element_type=jnp.float32) + jnp.dot(
        activated, w_fc2, preferred_element_type=jnp.float32
    )
    total = lax.psum(partial_value, "tensor")
    output = (widened + total + b_out + b_fc2).astype(jnp.bfloat16)
    g_bout = jnp.sum(cotangent.astype(jnp.float32), 0)
    g_w2 = jnp.dot(activated.T, cotangent, preferred_element_type=jnp.float32)
    dhidden = jnp.dot(cotangent, w_fc2.T, preferred_element_type=jnp.float32) * gelu_slope(
        hidden_pre
    )
    g_b1 = jnp.sum(dhidden, 0)
    dhidden_bf = dhidden.astype(jnp.bfloat16)
    g_w1 = jnp.dot(normed.T, dhidden_bf, preferred_element_type=jnp.float32)
    dnormed_local = jnp.dot(dhidden_bf, w_fc1.T, preferred_element_type=jnp.float32)
    g_wout = jnp.dot(attended.T, cotangent, preferred_element_type=jnp.float32)
    dattn_bf = (
        jnp.dot(cotangent, w_out.T, preferred_element_type=jnp.float32)
        .astype(jnp.bfloat16)
        .reshape(length, heads, HD)
    )
    delta = jnp.sum(
        dattn_bf.astype(jnp.float32) * attended.reshape(length, heads, HD).astype(jnp.float32), -1
    )
    dprob = jnp.einsum("qhd,khd->hqk", dattn_bf, value_bf, preferred_element_type=jnp.float32)
    dscore_bf = (probs * (dprob - jnp.transpose(delta)[:, :, None]) * HD ** (-0.5)).astype(
        jnp.bfloat16
    )
    dquery = jnp.einsum("hqk,khd->qhd", dscore_bf, key_rot, preferred_element_type=jnp.float32)
    dkey = jnp.einsum("hqk,qhd->khd", dscore_bf, query_rot, preferred_element_type=jnp.float32)
    dvalue = jnp.einsum("hqk,qhd->khd", prob_bf, dattn_bf, preferred_element_type=jnp.float32)
    dproj = jnp.stack(
        [unrotate(dquery, cosine, sine), unrotate(dkey, cosine, sine), dvalue], axis=2
    ).reshape(length, heads * 3 * HD)
    g_bqkv = jnp.sum(dproj, 0)
    dproj_bf = dproj.astype(jnp.bfloat16)
    g_wqkv = jnp.dot(normed.T, dproj_bf, preferred_element_type=jnp.float32)
    dnormed_local = dnormed_local + jnp.dot(dproj_bf, w_qkv.T, preferred_element_type=jnp.float32)
    dnormed = lax.psum(dnormed_local, "tensor")
    g_gain = jnp.sum(dnormed * normed_hat, 0)
    g_bias = jnp.sum(dnormed, 0)
    scaled = dnormed * ln_gain
    inner = (
        scaled
        - jnp.mean(scaled, -1, keepdims=True)
        - normed_hat * jnp.mean(scaled * normed_hat, -1, keepdims=True)
    )
    input_grad = cotangent.astype(jnp.float32) + inv_std * inner
    g_wqkv, g_bqkv, g_wout, g_bout, g_w1, g_b1, g_w2, g_gain, g_bias = lax.psum(
        (g_wqkv, g_bqkv, g_wout, g_bout, g_w1, g_b1, g_w2, g_gain, g_bias), "dp"
    )
    return (
        output,
        input_grad,
        g_gain,
        g_bias,
        g_wqkv,
        g_bqkv,
        g_wout,
        g_bout,
        g_w1,
        g_b1,
        g_w2,
        g_bout,
    )


def solution(mesh):
    placed = (
        P("dp", None),
        P(),
        P(),
        P(None, "tensor"),
        P("tensor"),
        P("tensor", None),
        P(),
        P(None, "tensor"),
        P("tensor"),
        P("tensor", None),
        P(),
        P("dp", None),
    )
    return jax.shard_map(
        per_device,
        mesh=mesh,
        in_specs=placed,
        out_specs=(
            P("dp", None),
            P("dp", None),
            P(),
            P(),
            P(None, "tensor"),
            P("tensor"),
            P("tensor", None),
            P(),
            P(None, "tensor"),
            P("tensor"),
            P("tensor", None),
            P(),
        ),
        check_vma=False,
    )
```

profile of v0, /device:TPU:0, one launch (start us, length us, event | category | flops | bytes accessed | tf_op | source)
XLA Modules:
  0.0 837.1 jit_solution(13396688774100656092)
XLA Ops:
  7.2 0.0 copy-start
  7.2 0.0 all-reduce.8.cloned.1.call-start
  7.2 0.0 copy-start.3
  7.3 1.6 convert_reduce_fusion
  8.9 1.6 fusion.12
  10.6 0.0 copy-start.2
  10.6 0.0 copy-start.28
  10.6 1.5 convolution_convert_fusion
  12.1 1.1 copy.49
  13.2 5.8 convolution_add_fusion.1
  19.0 3.0 copy.44
  22.0 1.3 fusion.42
  23.3 0.1 copy_bitcast_fusion
  23.5 0.1 multiply_cosine_fusion
  23.6 0.1 subtract_convert_fusion.1
  23.7 0.0 copy-start.6
  23.7 0.5 fusion.43
  24.2 0.3 exponential_reduce_fusion
  24.5 0.6 copy-done.6
  25.1 0.5 multiply_reduce_fusion.1
  25.6 0.5 convolution_bitcast_fusion
  26.1 0.0 slice-start.9
  26.1 0.7 multiply_convert_fusion
  26.8 0.4 convolution_bitcast_fusion.1
  27.2 0.3 convolution_bitcast_fusion.2
  27.5 0.0 slice-start.6
  27.5 0.1 multiply_add_fusion.2
  27.6 1.8 slice-done.9
  29.4 2.5 convolution_add_fusion.3
  32.0 2.6 fusion.36
  34.6 0.0 slice-start.4
  34.6 0.0 slice-start.5
  34.7 3.7 fusion.44
  38.5 0.9 copy-done.10
  39.4 0.1 fusion.23
  39.5 0.1 copy.54
  39.6 0.0 slice-start.11
  39.6 5.0 fusion.45
  44.7 2.1 convolution_add_fusion
  46.8 3.7 convolution_add_fusion.2
  50.5 0.0 all-reduce.8.cloned.1.call-update
  50.5 0.0 all-reduce.6.cloned.1.call-start
  50.6 1.1 copy-done.5
  51.7 0.0 copy-done.14
  51.7 2.7 fusion.46
  54.5 6.9 fusion.38
  61.4 8.7 %fusion.24 = f32[2048,2048]{1,0:T(8,128)} fusion(bf16[256,2048]{1,0:T(8,128)(2,1)S(1)} %copy-done.22, bf16[256,2048]{1,0:T(8,128)(2,1)S(1)} %copy-done.2, f32[2048]{0:T(1024)S(1)} %copy-done.24, f32[2048]{0:T(1024)S(1)} %copy-done.23, f32[256]{0:T(256)S(1)} %add_rsqrt_fusion, f32[256]{0:T(256)S(1)} %broadcast_multiply_fusion.2), kind=kOutput, calls=%fused_computation.54 | convolution fusion | flops 2150629376 | bytes 18892800 | tf_op jit(solution)/shard_map/dot_general | solution.py:96
  70.1 8.8 %fusion.35 = f32[2048,2048]{1,0:T(8,128)} fusion(bf16[256,2048]{1,0:T(8,128)(2,1)S(1)} %copy-done.5, f32[256,2048]{1,0:T(8,128)S(1)} %copy-done.18), kind=kOutput, calls=%fused_computation.83 | convolution fusion | flops 2152202240 | bytes 19922944 | tf_op jit(solution)/shard_map/dot_general | solution.py:90
  78.9 0.0 all-reduce.6.cloned.1.call-update
  79.0 1.0 copy-done.9
  80.0 0.2 copy-done.11
  80.1 1.4 fusion.22
  81.5 0.1 reduce_sum.110
  81.6 126.8 %all-reduce.8.cloned.1.call-done = (f32[256,2048]{1,0:T(8,128)}, f32[256,2048]{1,0:T(8,128)}) async-done(((f32[256,2048]{1,0:T(8,128)}, f32[256,2048]{1,0:T(8,128)}), (f32[256,2048]{1,0:T(8,128)}, f32[256,2048]{1,0:T(8,128)})) %all-reduce.8.cloned.1.call-update) | async-done | bytes 4194320 | tf_op jit(solution)/shard_map/psum | solution.py:87
  208.4 2.7 fusion.11
  211.1 4.8 convert_reduce_fusion.1
  215.9 27.2 %all-reduce = (f32[2048]{0:T(1024)}, f32[2048]{0:T(1024)}, f32[1536]{0:T(1024)}, f32[2048]{0:T(1024)S(1)}, f32[2048]{0:T(1024)}) all-reduce(f32[2048]{0:T(1024)S(1)} %get-tuple-element.12, f32[2048]{0:T(1024)S(1)} %get-tuple-element.15, f32[1536]{0:T(1024)S(1)} %reduce_sum.110, ...), channel_id=1, replica_groups=mesh['dp'=8,'tensor'=4] {'dp'}, use_global_device_ids=true, to_apply=%region_10.11 | all-reduce | flops 9728 | bytes 77824 | tf_op jit(solution)/shard_map/psum | solution.py:131
  243.1 549.5 %all-reduce.6.cloned.1.call-done = (f32[2048,1536]{1,0:T(8,128)}, f32[512,2048]{1,0:T(8,128)}, f32[2048,2048]{1,0:T(8,128)}, f32[2048,2048]{1,0:T(8,128)}) async-done(((f32[2048,1536]{1,0:T(8,128)}, f32[512,2048]{1,0:T(8,128)}, f32[2048,2048]{1,0:T(8,128)}, f32[2048,2048]{1,0:T(8,128)}), (f32[2048,1536]{1,0:T(8,128)}, f32[512,2048]{1,0:T(8,128)}, f32[2048,2048]{1,0:T(8,128)}, ...) | async-done | bytes 50331664 | tf_op jit(solution)/shard_map/psum | solution.py:131
  792.6 0.6 copy.80
  793.2 10.6 %copy.81 = f32[2048,1536]{1,0:T(8,128)} copy(f32[2048,1536]{1,0:T(8,128)} %get-tuple-element.84) | data formatting | bytes 25165824
  803.8 4.8 copy.82
  808.7 13.6 %copy.83 = f32[2048,2048]{1,0:T(8,128)} copy(f32[2048,2048]{1,0:T(8,128)} %get-tuple-element.88) | data formatting | bytes 33554432
  822.2 1.7 slice-done.3
  824.0 6.3 copy.84
  (83 shorter events, 0.3 us)
Async XLA Ops:
  7.2 3.4 copy-start
  7.2 201.2 %all-reduce.8.cloned.1.call-start = ((), (), s32[]{:S(2)}) async-start(), calls=%async_computation.1 | async-start | bytes 8388608 | tf_op jit(solution)/shard_map/psum | solution.py:87
  7.2 3.3 copy-start.3
  10.6 2.6 copy-start.2
  10.6 2.6 copy-start.23
  10.6 2.6 copy-start.24
  10.6 2.6 copy-start.28
  23.7 1.4 copy-start.6
  25.1 2.5 slice-start.8
  25.6 19.1 %copy-start.13 = (bf16[8,64,256]{2,1,0:T(8,128)(2,1)}, bf16[8,64,256]{2,1,0:T(8,128)(2,1)S(1)}, u32[]{:S(2)}) copy-start(bf16[8,64,256]{2,1,0:T(8,128)(2,1)S(1)} %get-tuple-element.49) | copy-start | bytes 786436
  26.1 12.4 %copy-start.12 = (f32[256,8,1,64]{0,3,1,2:T(8,128)}, f32[256,8,1,64]{0,3,1,2:T(8,128)S(1)}, u32[]{:S(2)}) copy-start(f32[256,8,1,64]{0,3,1,2:T(8,128)S(1)} %convolution_bitcast_fusion) | copy-start | bytes 1572868
  26.1 3.3 slice-start.9
  27.2 4.7 copy-start.19
  27.2 2.2 copy-start.29
  27.5 4.4 copy-start.20
  27.5 4.4 slice-start.6
  29.4 2.5 slice-start.7
  32.0 2.7 copy-start.17
  32.0 2.7 copy-start.4
  34.6 3.7 slice-start.4
  34.6 3.8 slice-start.5
  38.3 8.5 %copy-start.21 = (bf16[256,2048]{1,0:T(8,128)(2,1)}, bf16[256,2048]{1,0:T(8,128)(2,1)S(1)}, u32[]{:S(2)}) copy-start(bf16[256,2048]{1,0:T(8,128)(2,1)S(1)} %get-tuple-element.51) | copy-start | bytes 3145732
  38.4 1.2 copy-start.8
  38.5 0.9 copy-start.10
  39.4 7.4 slice-start.10
  39.6 5.1 copy-start.15
  39.6 7.2 slice-start.11
  50.5 1.2 copy-start.5
  50.5 1.3 copy-start.14
  50.5 4.0 copy-start.16
  50.5 742.1 %all-reduce.6.cloned.1.call-start = ((), (), s32[]{:S(2)}) async-start(), calls=%async_computation | async-start | bytes 100663296 | tf_op jit(solution)/shard_map/psum | solution.py:131
  54.5 6.9 copy-start.22
  61.4 8.7 %copy-start.18 = (f32[256,2048]{1,0:T(8,128)S(1)}, f32[256,2048]{1,0:T(8,128)}, u32[]{:S(2)}) copy-start(f32[256,2048]{1,0:T(8,128)} %copy-done.17) | copy-start | bytes 6291460
  78.9 1.0 copy-start.9
  78.9 1.2 copy-start.11
  80.1 131.0 %copy-start.26 = (f32[2048]{0:T(1024)S(1)}, f32[2048]{0:T(1024)}, u32[]{:S(2)}) copy-start(f32[2048]{0:T(1024)} %param.22) | copy-start | bytes 24580
  80.1 131.0 %copy-start.27 = (f32[2048]{0:T(1024)S(1)}, f32[2048]{0:T(1024)}, u32[]{:S(2)}) copy-start(f32[2048]{0:T(1024)} %param.18) | copy-start | bytes 24580
  208.4 2.7 copy-start.7
  243.1 560.7 %copy-start.25 = (f32[2048]{0:T(1024)}, f32[2048]{0:T(1024)S(1)}, u32[]{:S(2)}) copy-start(f32[2048]{0:T(1024)S(1)} %get-tuple-element.87) | copy-start | bytes 24580
  803.8 18.4 %slice-start = ((s8[16777216]{0:T(1024)(128)(4,1)}), s8[4194304]{0:T(1024)(128)(4,1)S(1)}, s32[]{:S(2)}) async-start(s8[16777216]{0:T(1024)(128)(4,1)} %bitcast.53), calls=%async_computation.2 | async-start | bytes 8388608
  808.7 13.6 %slice-start.1 = ((s8[16777216]{0:T(1024)(128)(4,1)}), s8[4194304]{0:T(1024)(128)(4,1)S(1)}, s32[]{:S(2)}) async-start(s8[16777216]{0:T(1024)(128)(4,1)} %bitcast.53), calls=%async_computation.3 | async-start | bytes 8388608
  808.7 13.6 %slice-start.2 = ((s8[16777216]{0:T(1024)(128)(4,1)}), s8[4194304]{0:T(1024)(128)(4,1)S(1)}, s32[]{:S(2)}) async-start(s8[16777216]{0:T(1024)(128)(4,1)} %bitcast.53), calls=%async_computation.4 | async-start | bytes 8388608
  808.7 15.3 %slice-start.3 = ((s8[16777216]{0:T(1024)(128)(4,1)}), s8[4194304]{0:T(1024)(128)(4,1)S(1)}, s32[]{:S(2)}) async-start(s8[16777216]{0:T(1024)(128)(4,1)} %bitcast.53), calls=%async_computation.5 | async-start | bytes 8388608
  824.0 6.3 copy-start.1
Sparse Core Ops, SparseCore 0:
  50.6 157.7 all-reduce.7
  213.8 578.7 all-reduce.5
where the time goes:
time: 838 us; the launch traced here: 837 us
  waiting for transfers between devices  676 us (81%)
  matrix products  56.8 us (7%)
  local copies, waits for them, and re-layouts  49.1 us (6%)
  blocking collectives  27.2 us (3%)
  between operations  14.7 us (2%)
  other arithmetic  13 us (2%)
    psum x1, waiting for transfers between devices, per_device(): lax.psum((g_wqkv, g_bqkv, g_wout, g_bout, g_w1, g_b1, g_w2, g_gain, g_bia...  549 us
    psum x1, waiting for transfers between devices, per_device(): total = lax.psum(partial_value, 'tensor')  127 us
    unnamed x85, local copies, waits for them, and re-layouts  43.4 us
    psum x1, blocking collectives, per_device(): lax.psum((g_wqkv, g_bqkv, g_wout, g_bout, g_w1, g_b1, g_w2, g_gain, g_bia...  27.2 us
  transfers between devices with their start and end apart: 2, of which 2 were waited for; matrix products, arithmetic and copies ran while one was open for 4% of the time, Pallas kernels for 0%

commit v1 on v0

--- a/solution.py
+++ b/solution.py
@@ -84,7 +84,7 @@
     partial_value = jnp.dot(attended, w_out, preferred_element_type=jnp.float32) + jnp.dot(
         activated, w_fc2, preferred_element_type=jnp.float32
     )
-    total = lax.psum(partial_value, "tensor")
+    total = jnp.sum(lax.all_gather(partial_value, "tensor"), axis=0)
     output = (widened + total + b_out + b_fc2).astype(jnp.bfloat16)
     g_bout = jnp.sum(cotangent.astype(jnp.float32), 0)
     g_w2 = jnp.dot(activated.T, cotangent, preferred_element_type=jnp.float32)

time: 838 us -> 916 us (1.093)
  waiting for transfers between devices: 676 us -> 742 us
    all_gather x0 -> x1, waiting for transfers between devices: none -> 148 us  [per_device(): total = jnp.sum(lax.all_gather(partial_value, 'tensor'), axis=0)]
    psum x1, waiting for transfers between devices: 127 us -> 49.4 us  [per_device(): dnormed = lax.psum(dnormed_local, 'tensor')]
    unnamed x85 -> x73, local copies, waits for them, and re-layouts: 43.4 us -> 44.8 us
  transfers between devices with their start and end apart: 2 -> 3, of which waited for: 2 -> 3; matrix products, arithmetic and copies ran while one was open for 4% -> 6% of each run, Pallas kernels for 0% -> 0%
where the time goes in v1:
time: 916 us
  waiting for transfers between devices  742 us (81%)
  matrix products  64.9 us (7%)
  local copies, waits for them, and re-layouts  50.6 us (6%)
  blocking collectives  27.5 us (3%)
  other arithmetic  16.4 us (2%)
  between operations  14.2 us (2%)
    psum x1, waiting for transfers between devices, per_device(): lax.psum((g_wqkv, g_bqkv, g_wout, g_bout, g_w1, g_b1, g_w2, g_gain, g_bia...  545 us
    all_gather x1, waiting for transfers between devices, per_device(): total = jnp.sum(lax.all_gather(partial_value, 'tensor'), axis=0)  148 us
    psum x1, waiting for transfers between devices, per_device(): dnormed = lax.psum(dnormed_local, 'tensor')  49.4 us
    unnamed x73, local copies, waits for them, and re-layouts  44.8 us
    psum x1, blocking collectives, per_device(): lax.psum((g_wqkv, g_bqkv, g_wout, g_bout, g_w1, g_b1, g_w2, g_gain, g_bia...  27.5 us
  transfers between devices with their start and end apart: 3, of which 3 were waited for; matrix products, arithmetic and copies ran while one was open for 6% of the time, Pallas kernels for 0%

profile of v1, /device:TPU:0, one launch (start us, length us, event | category | flops | bytes accessed | tf_op | source)
XLA Modules:
  0.0 915.9 jit_solution(17900054274490643689)
XLA Ops:
  7.2 0.0 copy-start
  7.2 0.0 all-reduce.5.cloned.1.call-start
  7.3 1.5 copy-done
  8.8 2.8 convolution_convert_fusion
  11.6 1.1 copy.49
  12.7 0.2 convert_reduce_fusion
  12.9 0.4 fusion.12
  13.4 5.8 convolution_add_fusion.1
  19.2 3.0 copy.44
  22.2 1.3 fusion.42
  23.5 0.1 copy_bitcast_fusion
  23.6 0.1 multiply_cosine_fusion
  23.8 0.1 subtract_convert_fusion.1
  23.9 0.0 copy-start.5
  23.9 0.5 fusion.43
  24.4 0.3 exponential_reduce_fusion
  24.7 0.6 copy-done.5
  25.3 1.2 multiply_reduce_fusion.1
  26.5 0.5 convolution_bitcast_fusion
  26.9 0.0 slice-start.6
  26.9 0.7 multiply_convert_fusion
  27.6 0.4 convolution_bitcast_fusion.1
  28.0 0.3 convolution_bitcast_fusion.2
  28.4 0.0 slice-start.7
  28.4 0.1 multiply_add_fusion.2
  28.6 0.0 slice-start.4
  28.6 0.8 copy-done.8
  29.4 0.1 fusion.23
  29.6 0.1 copy.54
  29.7 0.9 slice-done.7
  30.6 3.2 fusion.45
  33.8 2.5 convolution_add_fusion.3
  36.3 7.8 fusion.44
  44.1 1.0 copy-done.16
  45.1 3.7 convolution_add_fusion.2
  48.8 0.0 all-reduce.5.cloned.1.call-update
  48.8 0.0 all-gather.3.cloned.1.call-start
  48.9 6.6 fusion.36
  55.5 2.1 convolution_add_fusion
  57.6 0.0 all-gather.3.cloned.1.call-update
  57.6 0.0 all-reduce.7.cloned.1.call-start
  57.6 1.1 copy-done.4
  58.8 2.7 fusion.46
  61.5 6.8 fusion.38
  68.3 8.7 fusion.24
  77.0 8.8 fusion.35
  85.8 0.0 all-reduce.7.cloned.1.call-update
  85.8 1.0 copy-done.7
  86.9 0.2 copy-done.9
  87.0 1.3 fusion.22
  88.4 0.1 reduce_sum.120
  88.4 49.4 %all-reduce.5.cloned.1.call-done = f32[256,2048]{1,0:T(8,128)} async-done(((f32[256,2048]{1,0:T(8,128)}), f32[256,2048]{1,0:T(8,128)}) %all-reduce.5.cloned.1.call-update) | async-done | bytes 2097168 | tf_op jit(solution)/shard_map/psum | solution.py:121
  137.8 2.6 fusion.11
  140.4 147.7 %all-gather.3.cloned.1.call-done = f32[1024,2048]{1,0:T(8,128)} async-done(((f32[256,2048]{1,0:T(8,128)}), f32[1024,2048]{1,0:T(8,128)}) %all-gather.3.cloned.1.call-update) | async-done | bytes 8388624 | tf_op jit(solution)/shard_map/all_gather | solution.py:87
  288.1 5.7 reduce_sum.113
  293.8 5.4 convert_reduce_fusion.1
  299.2 27.5 %all-reduce = (f32[2048]{0:T(1024)}, f32[2048]{0:T(1024)}, f32[1536]{0:T(1024)}, f32[2048]{0:T(1024)S(1)}, f32[2048]{0:T(1024)}) all-reduce(f32[2048]{0:T(1024)S(1)} %get-tuple-element.12, f32[2048]{0:T(1024)S(1)} %get-tuple-element.15, f32[1536]{0:T(1024)S(1)} %reduce_sum.120, ...), channel_id=1, replica_groups=mesh['dp'=8,'tensor'=4] {'dp'}, use_global_device_ids=true, to_apply=%region_10.11 | all-reduce | flops 9728 | bytes 77824 | tf_op jit(solution)/shard_map/psum | solution.py:131
  326.6 545.0 %all-reduce.7.cloned.1.call-done = (f32[2048,1536]{1,0:T(8,128)}, f32[512,2048]{1,0:T(8,128)}, f32[2048,2048]{1,0:T(8,128)}, f32[2048,2048]{1,0:T(8,128)}) async-done(((f32[2048,1536]{1,0:T(8,128)}, f32[512,2048]{1,0:T(8,128)}, f32[2048,2048]{1,0:T(8,128)}, f32[2048,2048]{1,0:T(8,128)}), (f32[2048,1536]{1,0:T(8,128)}, f32[512,2048]{1,0:T(8,128)}, f32[2048,2048]{1,0:T(8,128)}, ...) | async-done | bytes 50331664 | tf_op jit(solution)/shard_map/psum | solution.py:131
  871.7 0.6 copy.79
  872.3 10.6 %copy.80 = f32[2048,1536]{1,0:T(8,128)} copy(f32[2048,1536]{1,0:T(8,128)} %get-tuple-element.82) | data formatting | bytes 25165824
  882.9 4.8 copy.81
  887.7 13.6 %copy.82 = f32[2048,2048]{1,0:T(8,128)} copy(f32[2048,2048]{1,0:T(8,128)} %get-tuple-element.86) | data formatting | bytes 33554432
  901.3 1.7 slice-done.3
  903.1 6.3 copy.83
  (72 shorter events, 0.3 us)
Async XLA Ops:
  7.2 1.6 copy-start
  7.2 130.6 %all-reduce.5.cloned.1.call-start = ((), (), s32[]{:S(2)}) async-start(), calls=%async_computation | async-start | bytes 4194304 | tf_op jit(solution)/shard_map/psum | solution.py:121
  8.8 3.9 copy-start.2
  11.5 1.8 copy-start.18
  11.5 1.8 copy-start.19
  11.6 1.8 copy-start.23
  23.9 1.4 copy-start.5
  26.9 1.7 copy-start.10
  26.9 2.7 slice-start.6
  28.4 2.2 slice-start.7
  28.5 1.1 copy-start.6
  28.6 5.2 slice-start.4
  28.6 0.8 copy-start.8
  29.7 4.1 copy-start.12
  30.6 3.2 slice-start.5
  30.6 3.2 copy-start.24
  33.8 2.5 copy-start.3
  36.3 7.8 copy-start.14
  36.3 8.8 copy-start.25
  44.1 1.0 copy-start.16
  48.8 6.7 copy-start.11
  48.8 239.3 %all-gather.3.cloned.1.call-start = ((), (), s32[]{:S(2)}) async-start(), calls=%async_computation.1 | async-start | bytes 10485760 | tf_op jit(solution)/shard_map/all_gather | solution.py:87
  57.6 1.2 copy-start.4
  57.6 3.9 copy-start.13
  57.6 814.1 %all-reduce.7.cloned.1.call-start = ((), (), s32[]{:S(2)}) async-start(), calls=%async_computation.2 | async-start | bytes 100663296 | tf_op jit(solution)/shard_map/psum | solution.py:131
  61.5 6.8 copy-start.17
  68.3 8.7 copy-start.15
  85.8 1.0 copy-start.7
  85.8 1.2 copy-start.9
  288.1 5.7 copy-start.21
  288.1 5.7 copy-start.22
  326.6 556.2 %copy-start.20 = (f32[2048]{0:T(1024)}, f32[2048]{0:T(1024)S(1)}, u32[]{:S(2)}) copy-start(f32[2048]{0:T(1024)S(1)} %get-tuple-element.85) | copy-start | bytes 24580
  882.9 18.4 %slice-start = ((s8[16777216]{0:T(1024)(128)(4,1)}), s8[4194304]{0:T(1024)(128)(4,1)S(1)}, s32[]{:S(2)}) async-start(s8[16777216]{0:T(1024)(128)(4,1)} %bitcast.54), calls=%async_computation.3 | async-start | bytes 8388608
  887.7 13.6 %slice-start.1 = ((s8[16777216]{0:T(1024)(128)(4,1)}), s8[4194304]{0:T(1024)(128)(4,1)S(1)}, s32[]{:S(2)}) async-start(s8[16777216]{0:T(1024)(128)(4,1)} %bitcast.54), calls=%async_computation.4 | async-start | bytes 8388608
  887.7 13.6 %slice-start.2 = ((s8[16777216]{0:T(1024)(128)(4,1)}), s8[4194304]{0:T(1024)(128)(4,1)S(1)}, s32[]{:S(2)}) async-start(s8[16777216]{0:T(1024)(128)(4,1)} %bitcast.54), calls=%async_computation.5 | async-start | bytes 8388608
  887.7 15.3 %slice-start.3 = ((s8[16777216]{0:T(1024)(128)(4,1)}), s8[4194304]{0:T(1024)(128)(4,1)S(1)}, s32[]{:S(2)}) async-start(s8[16777216]{0:T(1024)(128)(4,1)} %bitcast.54), calls=%async_computation.6 | async-start | bytes 8388608
  903.1 6.3 copy-start.1
Sparse Core Ops, SparseCore 0:
  48.9 88.8 all-reduce.4
  139.4 148.6 all-gather.2
  293.5 578.1 all-reduce.6
